TPU v7x, 128 devices: a whole 4x4x4 slice. The times are simulated.
128 devices in a mesh: ctx: 8 (over z_hi, x), tp: 8 (over y, core), ep: 2 (over z_lo).
Axes of the slice: x: 4, y: 4, z: 4 (z_hi: 2, z_lo: 2; z = z_hi * 2 + z_lo), core: 2. Of those that a mesh axis runs over, the one named last changes fastest.
Arguments:
- resid: bfloat16 [2048, 6144], P('ctx', ('tp', 'ep')), may hold values from -60 to 60
- queries: bfloat16 [2048, 6144], P('ctx', 'tp'), may hold values from -6 to 6
- keys: bfloat16 [2048, 1024], P('ctx', 'tp'), may hold values from -4 to 4
- values: bfloat16 [2048, 1024], P('ctx', 'tp'), may hold values from -5 to 5
- w_out: bfloat16 [6144, 6144], P('tp', ('ctx', 'ep')), may hold values from -0.078125 to 0.078125
- norm_gain: bfloat16 [6144], P(('tp', 'ep')), may hold values from 0.5 to 1.5
- w_gate: bfloat16 [8, 6144, 8192], P('tp', None, ('ctx', 'ep')), may hold values from -0.078125 to 0.078125
- w_up: bfloat16 [8, 6144, 8192], P('tp', None, ('ctx', 'ep')), may hold values from -0.078125 to 0.078125
- w_down: bfloat16 [8, 8192, 6144], P('tp', ('ctx', 'ep')), may hold values from -0.0625 to 0.0625
- expert_ids: int32 [2048, 2], P('ctx'), may hold values from 0 to 7, all different within a row; in each aligned block of 256 rows (0 to 255, 256 to 511, ...) at most 96 rows name the same one
- route_units: int32 [2048, 2], P('ctx'), may hold values from 1 to 65535
Outputs:
- mixed: bfloat16 [2048, 6144], P('ctx', ('tp', 'ep'))
Inputs may be any that keep to these rules, and one draw needn't show every extreme that they name: `expert_ids`: each row names two different experts; in every aligned block of 256 rows no expert is named by more than 96 rows, a bound that some block reaches.
All inputs are finite; a program needn't handle non-finite values.
Results may differ from a plain program's by a relative error of at most 0.01.
Values may be sent and summed in bfloat16 or wider, within the bound.
A program may use at most 128 MiB of HBM per device.

v0:
```python
import jax
import jax.numpy as jnp
from jax import lax
from jax.sharding import Mesh
from jax.sharding import PartitionSpec as P

D = 6144
HD = 128
TP = ("tp_0", "tp_1")
TP_EP = ("tp_0", "tp_1", "ep")


def split_up(x, dim, size):
    dims = x.shape
    tiles = x.reshape(*dims[:dim], size, dims[dim] // size, *dims[dim + 1 :])
    return jnp.moveaxis(tiles, dim, 0)


def sent_and_summed(x, axis, dim):
    tiles = split_up(x, dim, lax.axis_size(axis))
    arrived = lax.all_to_all(tiles, axis, split_axis=0, concat_axis=0, tiled=True)
    return arrived.astype(jnp.float32).sum(axis=0)


def from_everyone(x, axis):
    size = lax.axis_size(axis)
    return lax.all_to_all(jnp.broadcast_to(x[None], (size, *x.shape)), axis, 0, 0, tiled=True)


def taken_together(x, axis):
    everything = from_everyone(x, axis)
    return jnp.sum(everything, axis=0)


def laid_out(tiles, dim):
    dims = list(tiles.shape[1:])
    dims[dim] *= tiles.shape[0]
    return jnp.moveaxis(tiles, 0, dim).reshape(dims)


def moved_by_axis(tiles, axes, sequence):
    dims = [lax.axis_size(a) for a in axes]
    tiles = tiles.reshape(*dims, *tiles.shape[1:])
    for k in sequence:
        tiles = lax.all_to_all(tiles, axes[k], split_axis=k, concat_axis=k, tiled=True)
    return tiles.reshape(-1, *tiles.shape[len(axes) :])


def one_axis_at_a_time(x, axes, sequence, split_dim, concat_dim):
    tiles = split_up(x, split_dim, lax.axis_size(axes))
    return laid_out(moved_by_axis(tiles, axes, sequence), concat_dim)


def from_partner(x, axis, distance):
    return lax.ppermute(x, axis, [(i, i ^ 1 << distance) for i in range(lax.axis_size(axis))])


def on_device(
    resid, queries, keys, values, w_out, norm_gain, w_gate, w_up, w_down, expert_ids, route_units
):
    tp_size = lax.axis_size(TP)
    ep_size = lax.axis_size("ep")
    ctx_size = lax.axis_size("ctx")
    tok_rows = queries.shape[0]
    heads_dev = queries.shape[1] // HD
    kv_dev = keys.shape[1] // HD
    group = heads_dev // kv_dev
    feat_dev = resid.shape[1]
    hidden_dev = w_gate.shape[2]
    capacity = 3 * tok_rows // tp_size
    first_pos = lax.axis_index("ctx") * tok_rows
    query_heads = queries.reshape(tok_rows, kv_dev, group, HD)
    query_pos = first_pos + jnp.arange(tok_rows, dtype=jnp.int32)
    running_max = jnp.full((kv_dev, group, tok_rows), -1e30, jnp.float32)
    key_piece = lax.all_gather(keys, "ctx", axis=0, tiled=True)
    value_piece = lax.all_gather(values, "ctx", axis=0, tiled=True)
    count = key_piece.shape[0]
    key_rows = key_piece.reshape(count, kv_dev, HD)
    value_rows = value_piece.reshape(count, kv_dev, HD)
    scores = jnp.einsum(
        "tkgd,nkd->kgtn", query_heads, key_rows, preferred_element_type=jnp.float32
    ) * HD ** (-0.5)
    key_pos = jnp.arange(count, dtype=jnp.int32)
    allowed = (key_pos[None, :] <= query_pos[:, None])[None, None]
    block_max = jnp.max(jnp.where(allowed, scores, -1e30), axis=-1)
    new_max = jnp.maximum(running_max, block_max)
    probs = jnp.where(allowed, jnp.exp(scores - new_max[..., None]), 0.0)
    new_sum = jnp.sum(probs, axis=-1)
    probs_b = probs.astype(jnp.bfloat16)
    update = jnp.einsum("kgtn,nkd->kgtd", probs_b, value_rows, preferred_element_type=jnp.float32)
    attn = (
        (update / new_sum[..., None])
        .transpose(2, 0, 1, 3)
        .reshape(tok_rows, heads_dev * HD)
        .astype(jnp.bfloat16)
    )
    partial_proj = jnp.dot(
        attn, lax.all_gather(w_out, "ctx", axis=1, tiled=True), preferred_element_type=jnp.float32
    )
    proj = sent_and_summed(partial_proj.astype(jnp.bfloat16), TP, 1)
    hres = (resid.astype(jnp.float32) + proj).astype(jnp.bfloat16)
    hfloat = hres.astype(jnp.float32)
    square_total = taken_together(jnp.sum(hfloat * hfloat, axis=1, keepdims=True), TP_EP)
    normed = (hfloat * lax.rsqrt(square_total / D + 1e-05) * norm_gain.astype(jnp.float32)).astype(
        jnp.bfloat16
    )
    onehot = (expert_ids[..., None] == jnp.arange(tp_size, dtype=jnp.int32)).astype(jnp.int32)
    per_token = jnp.sum(onehot, axis=1)
    earlier = jnp.cumsum(per_token, axis=0) - per_token
    slot = jnp.sum(onehot * earlier[:, None, :], axis=-1)
    codes = expert_ids * capacity + slot
    slot_ids = jnp.arange(tp_size * capacity, dtype=jnp.int32)
    picks = (
        (slot_ids[:, None] == codes[None, :, 0]) | (slot_ids[:, None] == codes[None, :, 1])
    ).astype(jnp.bfloat16)
    dispatched = jnp.dot(picks, normed, preferred_element_type=jnp.float32).astype(jnp.bfloat16)
    dispatched = dispatched.reshape(tp_size, 1, capacity, feat_dev)
    arrived = one_axis_at_a_time(dispatched, TP, (1, 0), 0, 1)
    gate_w = w_gate[0].reshape(tp_size, ep_size, feat_dev, hidden_dev)
    up_w = w_up[0].reshape(tp_size, ep_size, feat_dev, hidden_dev)
    zero_acc = jnp.zeros((ctx_size, capacity, hidden_dev), jnp.float32)
    piece = lax.all_gather(arrived, ("ctx", "ep"), axis=0, tiled=True)

    def one_row(index, totals):
        gate_total, up_total = totals
        source = index // ep_size
        parity = index % ep_size
        row = lax.dynamic_index_in_dim(piece, index, 0, keepdims=False)
        gate_part = lax.dynamic_index_in_dim(gate_w, parity, 1, keepdims=False)
        up_part = lax.dynamic_index_in_dim(up_w, parity, 1, keepdims=False)
        gate_add = jnp.einsum("tsj,tjf->sf", row, gate_part, preferred_element_type=jnp.float32)
        up_add = jnp.einsum("tsj,tjf->sf", row, up_part, preferred_element_type=jnp.float32)
        gate_now = lax.dynamic_index_in_dim(gate_total, source, 0, keepdims=False) + gate_add
        up_now = lax.dynamic_index_in_dim(up_total, source, 0, keepdims=False) + up_add
        return (
            lax.dynamic_update_index_in_dim(gate_total, gate_now, source, 0),
            lax.dynamic_update_index_in_dim(up_total, up_now, source, 0),
        )

    gate_acc, up_acc = lax.fori_loop(0, piece.shape[0], one_row, (zero_acc, zero_acc))
    hidden = (jax.nn.silu(gate_acc) * up_acc).astype(jnp.bfloat16)
    down_w = w_down[0].reshape(hidden_dev, tp_size, ep_size, feat_dev)
    parity = lax.axis_index("ep")
    mine_cols = lax.dynamic_index_in_dim(down_w, parity, 2, keepdims=False)
    give_cols = lax.dynamic_index_in_dim(down_w, 1 - parity, 2, keepdims=False)
    got_hidden, got_cols = from_partner((hidden, give_cols), "ep", 0)
    hidden_both = jnp.concatenate([hidden, got_hidden], axis=2)
    cols_both = jnp.concatenate([mine_cols, got_cols], axis=0)
    blocks = lax.axis_size("ctx") * capacity // capacity
    product = jnp.einsum(
        "csf,ftj->cstj", hidden_both, cols_both, preferred_element_type=jnp.float32
    )
    expert_sum = lax.psum_scatter(
        product.reshape(blocks * capacity, tp_size * feat_dev).astype(jnp.bfloat16),
        "ctx",
        scatter_dimension=0,
        tiled=True,
    )
    expert_out = expert_sum.reshape(1, capacity, tp_size, feat_dev)
    returned = lax.all_to_all(expert_out, TP, split_axis=2, concat_axis=0, tiled=True)
    units = route_units.astype(jnp.float32)
    weights = (units / jnp.sum(units, axis=-1, keepdims=True)).astype(jnp.bfloat16)
    combine = jnp.where(slot_ids[None, :] == codes[:, 0:1], weights[:, 0:1], 0.0) + jnp.where(
        slot_ids[None, :] == codes[:, 1:2], weights[:, 1:2], 0.0
    )
    moe = jnp.dot(
        combine, returned.reshape(tp_size * capacity, feat_dev), preferred_element_type=jnp.float32
    )
    return (hfloat + moe).astype(jnp.bfloat16)


def solution(mesh):
    torus = Mesh(
        mesh.devices.reshape(mesh.shape["ctx"], 4, 2, mesh.shape["ep"]),
        ("ctx", "tp_0", "tp_1", "ep"),
    )
    in_specs = (
        P("ctx", TP_EP),
        P("ctx", TP),
        P("ctx", TP),
        P("ctx", TP),
        P(TP, ("ctx", "ep")),
        P(TP_EP),
        P(TP, None, ("ctx", "ep")),
        P(TP, None, ("ctx", "ep")),
        P(TP, ("ctx", "ep"), None),
        P("ctx", None),
        P("ctx", None),
    )
    out_specs = P("ctx", TP_EP)
    return jax.shard_map(
        on_device, mesh=torus, in_specs=in_specs, out_specs=out_specs, check_vma=False
    )
```

profile of v0, /device:TPU:1, one launch (start us, length us, event | category | flops | bytes accessed | tf_op | source)
XLA Modules:
  0.0 661.8 jit_solution(15073614211163878347)
XLA Ops:
  7.3 1.2 copy.45
  8.4 0.9 copy.47
  9.4 31.8 %all_gather.12 = bf16[2048,128]{1,0:T(8,128)(2,1)S(1)} all-gather(bf16[256,128]{1,0:T(8,128)(2,1)} %param.15), channel_id=1, replica_groups=mesh['ctx'=8,'tp_0'=4,'tp_1'=2,'ep'=2] {'ctx'}, dimensions={0}, use_global_device_ids=true | all-gather | bytes 589824 | tf_op jit(solution)/shard_map/all_gather | solution.py:75
  41.6 2.0 fusion.36
  43.6 30.6 %all_gather.13 = bf16[2048,128]{0,1:T(8,128)(2,1)S(1)} all-gather(bf16[256,128]{0,1:T(8,128)(2,1)S(1)} %copy.47), channel_id=1, replica_groups=mesh['ctx'=8,'tp_0'=4,'tp_1'=2,'ep'=2] {'ctx'}, dimensions={0}, use_global_device_ids=true | all-gather | bytes 589824 | tf_op jit(solution)/shard_map/all_gather | solution.py:76
  74.3 2.6 fusion.39
  76.9 2.9 fusion.55
  79.8 19.2 %all-gather.3.cloned.1.call-done = bf16[768,3072]{1,0:T(8,128)(2,1)} async-done(((bf16[768,384]{1,0:T(8,128)(2,1)}), bf16[768,3072]{1,0:T(8,128)(2,1)}) %all-gather.3.cloned.1.call-update) | async-done | bytes 4718608 | tf_op jit(solution)/shard_map/all_gather | solution.py:98
  99.0 3.8 convolution_convert_fusion
  102.8 1.3 copy.73
  104.1 5.7 all-to-all-start
  110.7 19.6 %all-to-all-done = bf16[8,256,384]{2,1,0:T(8,128)(2,1)S(1)} async-done(((bf16[8,256,384]{2,1,0:T(8,128)(2,1)}), bf16[8,256,384]{2,1,0:T(8,128)(2,1)S(1)}, u32[]{:S(2)}, u32[]{:S(2)}) %all-to-all-start) | async-done | bytes 1572896 | tf_op jit(solution)/shard_map/all_to_all | solution.py:21
  131.4 4.3 all-to-all-start.1
  135.7 5.8 all-to-all-done.1
  142.2 4.2 all_to_all.35
  146.4 12.7 %all_to_all.36 = bf16[4,2,1,1,96,384]{5,4,1,3,2,0:T(8,128)(2,1)} all-to-all(bf16[4,2,1,1,96,384]{5,4,1,3,2,0:T(8,128)(2,1)S(1)} %copy.51), channel_id=1, replica_groups=mesh['ctx'=8,'tp_0'=4,'tp_1'=2,'ep'=2] {'tp_0'}, dimensions={0} | all-to-all | bytes 1179648 | tf_op jit(solution)/shard_map/all_to_all | solution.py:45
  159.4 14.6 %reshape_squeeze.11 = bf16[512,8,2,384]{3,2,1,0:T(2,128)(2,1)} reshape(bf16[1,512,6144]{2,1,0:T(8,128)(2,1)} %param.21) | data formatting | bytes 12582912 | tf_op jit(solution)/shard_map/reshape;squeeze | solution.py:142
  174.0 15.4 %constant_dynamic-slice_fusion.3 = (bf16[512,8,1,384]{3,2,1,0:T(2,128)(2,1)}, bf16[512,8,1,384]{3,2,1,0:T(2,128)(2,1)S(1)}) fusion(bf16[512,8,2,384]{3,2,1,0:T(2,128)(2,1)} %reshape_squeeze.11, s32[]{:T(128)S(6)} %select_n.93, s32[]{:T(128)S(6)} %select_n.94), kind=kLoop, calls=%fused_computation.93 | loop fusion | bytes 12582920 | tf_op jit(solution)/shard_map/jit(dynamic_index_in_dim)/dynamic_slice | solution.py:144
  189.4 2.8 copy.71
  192.5 226.1 %all-gather.5.cloned.1.call-done = bf16[16,8,96,384]{3,2,1,0:T(8,128)(2,1)} async-done(((bf16[1,8,96,384]{3,2,1,0:T(8,128)(2,1)}), bf16[16,8,96,384]{3,2,1,0:T(8,128)(2,1)}) %all-gather.5.cloned.1.call-update) | async-done | bytes 9437200 | tf_op jit(solution)/shard_map/all_gather | solution.py:122
  419.0 88.4 %while.17 = (s32[]{:T(128)}, f32[8,96,512]{2,1,0:T(8,128)S(1)}, f32[8,96,512]{2,1,0:T(8,128)S(1)}, bf16[16,8,96,384]{3,2,1,0:T(8,128)(2,1)}, bf16[8,2,384,512]{3...) while((s32[]{:T(128)}, f32[8,96,512]{2,1,0:T(8,128)S(1)}, ...), condition=%wide.region_11.12_spmd, body=%wide.region_10.11_spmd.sunk | while | flops 604078080 | bytes 9045304 | solution.py:140
  419.1 2.7 fusion.102
  421.8 2.7 fusion.101
  424.6 2.7 fusion.102
  427.3 2.7 fusion.101
  430.1 2.7 fusion.102
  432.8 2.7 fusion.101
  435.6 2.7 fusion.102
  438.4 2.7 fusion.101
  441.2 2.7 fusion.102
  443.9 2.7 fusion.101
  446.7 2.7 fusion.102
  449.4 2.7 fusion.101
  452.2 2.7 fusion.102
  454.9 2.7 fusion.101
  457.7 2.7 fusion.102
  460.5 2.7 fusion.101
  463.3 2.7 fusion.102
  466.0 2.7 fusion.101
  468.8 2.7 fusion.102
  471.5 2.7 fusion.101
  474.3 2.7 fusion.102
  477.0 2.7 fusion.101
  479.8 2.7 fusion.102
  482.5 2.7 fusion.101
  485.3 2.7 fusion.102
  488.1 2.7 fusion.101
  490.9 2.7 fusion.102
  493.6 2.7 fusion.101
  496.4 2.7 fusion.102
  499.1 2.7 fusion.101
  501.9 2.7 fusion.102
  504.6 2.7 fusion.101
  507.8 7.8 %collective-permute-start = (bf16[8,96,512]{2,1,0:T(8,128)(2,1)S(1)}, bf16[8,96,512]{2,1,0:T(8,128)(2,1)S(1)}, u32[]{:S(2)}, u32[]{:S(2)}) collective-permute-start(bf16[8,96,512]{2,1,0:T(8,128)(2,1)S(1)} %multiply_convert_fusion), channel_id=1, source_target_pairs={{0,1},{1,0},{2,3},{3,2},{4,5},{5,4},{6,7},{7,6},{8,9},{9,8},{10,11... | collective-permute-start | bytes 2359304 | tf_op jit(solution)/shard_map/ppermute | solution.py:55
  515.6 3.9 copy.72
  519.5 13.0 %collective-permute-done = bf16[8,96,512]{2,1,0:T(8,128)(2,1)S(1)} collective-permute-done((bf16[8,96,512]{2,1,0:T(8,128)(2,1)S(1)}, bf16[8,96,512]{2,1,0:T(8,128)(2,1)S(1)}, u32[]{:S(2)}, u32[]{:S(2)}) %collective-permute-start) | collective-permute-done | bytes 786464 | tf_op jit(solution)/shard_map/ppermute | solution.py:55
  532.6 6.7 %fusion.48 = bf16[8,96,8,384]{3,1,2,0:T(8,128)(2,1)S(1)} fusion(bf16[512,8,384]{2,0,1:T(8,128)(2,1)} %collective-permute-done.1, bf16[512,8,384]{2,0,1:T(8,128)(2,1)S(1)} %bitcast.178, bf16[8,96,512]{2,1,0:T(8,128)(2,1)S(1)} %collective-permute-done, bf16[8,96,512]{2,1,0:T(8,128)(2,1)S(1)} %multiply_convert_fusion), kind=kOutput, calls=%fused_computation.40 | convolution fusion | flops 4849926144 | bytes 12582912 | tf_op jit(solution)/shard_map/csf,ftj->cstj/dot_general | solution.py:150
  539.2 1.9 copy.56
  541.1 3.3 copy.66
  544.5 91.3 %reduce-scatter.2.cloned.1.call-done = bf16[96,3072]{1,0:T(8,128)(2,1)} async-done(((bf16[768,3072]{1,0:T(8,128)(2,1)}), bf16[96,3072]{1,0:T(8,128)(2,1)}) %reduce-scatter.2.cloned.1.call-update) | async-done | bytes 589840 | tf_op jit(solution)/shard_map/reduce_scatter | solution.py:153
  635.7 1.1 copy.67
  637.8 6.2 all-to-all-start.4
  644.1 10.0 %all-to-all-done.4 = bf16[1,96,8,384]{3,1,0,2:T(8,128)(2,1)S(1)} async-done(((bf16[1,96,8,384]{3,1,0,2:T(8,128)(2,1)}), bf16[1,96,8,384]{3,1,0,2:T(8,128)(2,1)S(1)}, u32[]{:S(2)}, u32[]{:S(2)}) %all-to-all-start.4) | async-done | bytes 589856 | tf_op jit(solution)/shard_map/all_to_all | solution.py:160
  654.1 1.2 fusion.51
  (64 shorter events, 6.5 us)
Async XLA Ops:
  6.5 92.4 %all-gather.3.cloned.1.call-start = ((), (), s32[]{:S(2)}) async-start(), calls=%async_computation.6 | async-start | bytes 5308416 | tf_op jit(solution)/shard_map/all_gather | solution.py:98
  102.7 7.1 %copy-start.3 = (s32[256,2]{0,1:T(2,128)S(1)}, s32[256,2]{0,1:T(2,128)}, u32[]{:S(2)}) copy-start(s32[256,2]{0,1:T(2,128)} %param.22) | copy-start | bytes 6148
  102.7 27.8 %copy-start = (bf16[256,384]{1,0:T(8,128)(2,1)S(1)}, bf16[256,384]{1,0:T(8,128)(2,1)}, u32[]{:S(2)}) copy-start(bf16[256,384]{1,0:T(8,128)(2,1)} %param.13) | copy-start | bytes 589828
  102.7 33.0 %copy-start.5 = (bf16[384]{0:T(512)(128)(2,1)S(1)}, bf16[384]{0:T(512)(128)(2,1)}, u32[]{:S(2)}) copy-start(bf16[384]{0:T(512)(128)(2,1)} %param.18) | copy-start | bytes 2308
  104.1 26.3 %all-to-all-start = ((bf16[8,256,384]{2,1,0:T(8,128)(2,1)}), bf16[8,256,384]{2,1,0:T(8,128)(2,1)S(1)}, u32[]{:S(2)}, u32[]{:S(2)}) async-start(bf16[8,256,384]{2,1,0:T(8,128)(2,1)} %bitcast.152), calls=%async_computation | async-start | bytes 3145728 | tf_op jit(solution)/shard_map/all_to_all | solution.py:21
  130.7 43.3 %copy-start.1 = (bf16[256,384]{1,0:T(8,128)(2,1)}, bf16[256,384]{1,0:T(8,128)(2,1)S(1)}, u32[]{:S(2)}) copy-start(bf16[256,384]{1,0:T(8,128)(2,1)S(1)} %get-tuple-element.198) | copy-start | bytes 589828
  131.4 10.2 %all-to-all-start.1 = ((f32[16,256,1]{1,2,0:T(1,128)}), f32[16,256,1]{1,2,0:T(1,128)S(1)}, u32[]{:S(2)}, u32[]{:S(2)}) async-start(f32[16,256,1]{1,2,0:T(1,128)} %broadcast_in_dim.96), calls=%async_computation.1 | async-start | bytes 32768 | tf_op jit(solution)/shard_map/all_to_all | solution.py:27
  135.7 282.9 %all-gather.5.cloned.1.call-start = ((), (), s32[]{:S(2)}) async-start(), calls=%async_computation.7 | async-start | bytes 10027008 | tf_op jit(solution)/shard_map/all_gather | solution.py:122
  159.2 476.6 %reduce-scatter.2.cloned.1.call-start = ((), (), s32[]{:S(2)}) async-start(), calls=%async_computation.8 | async-start | bytes 5308416 | tf_op jit(solution)/shard_map/reduce_scatter | solution.py:153
  192.2 327.3 %collective-permute-start.1 = (bf16[512,8,384]{2,0,1:T(8,128)(2,1)}, bf16[512,8,384]{2,0,1:T(8,128)(2,1)}, u32[]{:S(2)}, u32[]{:S(2)}) collective-permute-start(bf16[512,8,384]{2,0,1:T(8,128)(2,1)} %bitcast.149), channel_id=1, source_target_pairs={{0,1},{1,0},{2,3},{3,2},{4,5},{5,4},{6,7},{7,6},{8,9},{9,8},{10,11... | collective-permute-start | bytes 9437192 | tf_op jit(solution)/shard_map/ppermute | solution.py:55
  507.8 24.7 %collective-permute-start = (bf16[8,96,512]{2,1,0:T(8,128)(2,1)S(1)}, bf16[8,96,512]{2,1,0:T(8,128)(2,1)S(1)}, u32[]{:S(2)}, u32[]{:S(2)}) collective-permute-start(bf16[8,96,512]{2,1,0:T(8,128)(2,1)S(1)} %multiply_convert_fusion), channel_id=1, source_target_pairs={{0,1},{1,0},{2,3},{3,2},{4,5},{5,4},{6,7},{7,6},{8,9},{9,8},{10,11... | collective-permute-start | bytes 2359304 | tf_op jit(solution)/shard_map/ppermute | solution.py:55
  544.4 99.6 %copy-start.4 = (s32[256,2]{0,1:T(2,128)S(1)}, s32[256,2]{0,1:T(2,128)}, u32[]{:S(2)}) copy-start(s32[256,2]{0,1:T(2,128)} %param.23) | copy-start | bytes 6148
  544.4 109.6 %copy-start.2 = (bf16[256,384]{1,0:T(8,128)(2,1)S(1)}, bf16[256,384]{1,0:T(8,128)(2,1)}, u32[]{:S(2)}) copy-start(bf16[256,384]{1,0:T(8,128)(2,1)} %copy-done.1) | copy-start | bytes 589828
  637.8 16.3 %all-to-all-start.4 = ((bf16[1,96,8,384]{3,1,0,2:T(8,128)(2,1)}), bf16[1,96,8,384]{3,1,0,2:T(8,128)(2,1)S(1)}, u32[]{:S(2)}, u32[]{:S(2)}) async-start(bf16[1,96,8,384]{3,1,0,2:T(8,128)(2,1)} %copy.57), calls=%async_computation.5 | async-start | bytes 1179648 | tf_op jit(solution)/shard_map/all_to_all | solution.py:160
Sparse Core Ops, SparseCore 0:
  9.5 89.3 all-gather.2
  159.3 259.2 all-gather.4
  544.6 91.1 reduce-scatter.1
where the time goes:
time: 663 us; the launch traced here: 662 us
  waiting for transfers between devices  386 us (58%)
  matrix products  104 us (16%)
  blocking collectives  79.4 us (12%)
  local copies, waits for them, and re-layouts  49.3 us (7%)
  starting transfers between devices  24.5 us (4%)
  between operations  13.4 us (2%)
    all_gather x1, waiting for transfers between devices, on_device(): piece = lax.all_gather(arrived, ('ctx', 'ep'), axis=0, tiled=True)  226 us
    reduce_scatter x1, waiting for transfers between devices, on_device(): lax.psum_scatter(product.reshape(blocks * capacity, tp_size * feat_dev).a...  91.3 us
    dot_general x16, matrix products, one_row(): jnp.einsum('tsj,tjf->sf', row, gate_part, preferred_element_type=jnp.floa...  43.6 us
    dot_general x16, matrix products, one_row(): jnp.einsum('tsj,tjf->sf', row, up_part, preferred_element_type=jnp.float32)  43.5 us
    all_gather x1, blocking collectives, on_device(): key_piece = lax.all_gather(keys, 'ctx', axis=0, tiled=True)  31.8 us
    all_gather x1, blocking collectives, on_device(): value_piece = lax.all_gather(values, 'ctx', axis=0, tiled=True)  30.6 us
    all_to_all x1, waiting for transfers between devices, sent_and_summed(): lax.all_to_all(tiles, axis, split_axis=0, concat_axis=0, tiled=True)  19.6 us
    all_gather x1, waiting for transfers between devices, on_device(): lax.all_gather(w_out, 'ctx', axis=1, tiled=True)  19.2 us
  transfers between devices with their start and end apart: 8, of which 7 were waited for; matrix products, arithmetic and copies ran while one was open for 21% of the time, Pallas kernels for 0%

commit v1 on v0

--- a/solution.py
+++ b/solution.py
@@ -119,7 +119,10 @@
     gate_w = w_gate[0].reshape(tp_size, ep_size, feat_dev, hidden_dev)
     up_w = w_up[0].reshape(tp_size, ep_size, feat_dev, hidden_dev)
     zero_acc = jnp.zeros((ctx_size, capacity, hidden_dev), jnp.float32)
-    piece = lax.all_gather(arrived, ("ctx", "ep"), axis=0, tiled=True)
+    piece = jnp.concatenate(
+        lax.all_to_all(jnp.stack([arrived] * lax.axis_size(("ctx", "ep"))), ("ctx", "ep"), 0, 0),
+        axis=0,
+    )
 
     def one_row(index, totals):
         gate_total, up_total = totals

time: 663 us -> 538 us (0.81)
  waiting for transfers between devices: 386 us -> 257 us
    all_gather x1 -> x0, waiting for transfers between devices: 226 us -> none  [on_device(): piece = lax.all_gather(arrived, ('ctx', 'ep'), axis=0, tiled=True)]
    all_to_all x0 -> x1, waiting for transfers between devices: none -> 102 us  [on_device(): lax.all_to_all(jnp.stack([arrived] * lax.axis_size(('ctx', 'ep'))), ('ctx...]
  transfers between devices with their start and end apart: 8 -> 8, of which waited for: 7 -> 7; matrix products, arithmetic and copies ran while one was open for 21% -> 25% of each run, Pallas kernels for 0% -> 0%
where the time goes in v1:
time: 538 us; the launch traced here: 537 us
  waiting for transfers between devices  257 us (48%)
  matrix products  104 us (19%)
  blocking collectives  78.7 us (15%)
  local copies, waits for them, and re-layouts  54.2 us (10%)
  starting transfers between devices  23.7 us (4%)
  between operations  13.7 us (3%)
    all_to_all x1, waiting for transfers between devices, on_device(): lax.all_to_all(jnp.stack([arrived] * lax.axis_size(('ctx', 'ep'))), ('ctx...  102 us
    reduce_scatter x1, waiting for transfers between devices, on_device(): lax.psum_scatter(product.reshape(blocks * capacity, tp_size * feat_dev).a...  88.1 us
    dot_general x16, matrix products, one_row(): jnp.einsum('tsj,tjf->sf', row, gate_part, preferred_element_type=jnp.floa...  43.6 us
    dot_general x16, matrix products, one_row(): jnp.einsum('tsj,tjf->sf', row, up_part, preferred_element_type=jnp.float32)  43.5 us
    all_gather x1, blocking collectives, on_device(): key_piece = lax.all_gather(keys, 'ctx', axis=0, tiled=True)  31.8 us
    all_gather x1, blocking collectives, on_device(): value_piece = lax.all_gather(values, 'ctx', axis=0, tiled=True)  30.6 us
    all_to_all x1, waiting for transfers between devices, sent_and_summed(): lax.all_to_all(tiles, axis, split_axis=0, concat_axis=0, tiled=True)  19.6 us
    all_gather x1, waiting for transfers between devices, on_device(): lax.all_gather(w_out, 'ctx', axis=1, tiled=True)  19.2 us
  transfers between devices with their start and end apart: 8, of which 7 were waited for; matrix products, arithmetic and copies ran while one was open for 25% of the time, Pallas kernels for 0%

profile of v1, /device:TPU:1, one launch (start us, length us, event | category | flops | bytes accessed | tf_op | source)
XLA Modules:
  0.0 536.5 jit_solution(15525446918843746384)
XLA Ops:
  7.3 1.2 copy.45
  9.4 31.8 %all_gather.9 = bf16[2048,128]{1,0:T(8,128)(2,1)S(1)} all-gather(bf16[256,128]{1,0:T(8,128)(2,1)} %param.15), channel_id=1, replica_groups=mesh['ctx'=8,'tp_0'=4,'tp_1'=2,'ep'=2] {'ctx'}, dimensions={0}, use_global_device_ids=true | all-gather | bytes 589824 | tf_op jit(solution)/shard_map/all_gather | solution.py:75
  41.6 2.0 fusion.36
  43.6 30.6 %all_gather.10 = bf16[2048,128]{0,1:T(8,128)(2,1)S(1)} all-gather(bf16[256,128]{0,1:T(8,128)(2,1)S(1)} %copy.47), channel_id=1, replica_groups=mesh['ctx'=8,'tp_0'=4,'tp_1'=2,'ep'=2] {'ctx'}, dimensions={0}, use_global_device_ids=true | all-gather | bytes 589824 | tf_op jit(solution)/shard_map/all_gather | solution.py:76
  74.3 2.6 fusion.39
  76.9 2.9 fusion.55
  79.8 19.2 %all-gather.2.cloned.1.call-done = bf16[768,3072]{1,0:T(8,128)(2,1)} async-done(((bf16[768,384]{1,0:T(8,128)(2,1)}), bf16[768,3072]{1,0:T(8,128)(2,1)}) %all-gather.2.cloned.1.call-update) | async-done | bytes 4718608 | tf_op jit(solution)/shard_map/all_gather | solution.py:98
  99.0 3.8 convolution_convert_fusion
  102.8 1.3 copy.73
  104.1 5.7 %all-to-all-start = ((bf16[8,256,384]{2,1,0:T(8,128)(2,1)}), bf16[8,256,384]{2,1,0:T(8,128)(2,1)S(1)}, u32[]{:S(2)}, u32[]{:S(2)}) async-start(bf16[8,256,384]{2,1,0:T(8,128)(2,1)} %bitcast.153), calls=%async_computation | async-start | bytes 3145728 | tf_op jit(solution)/shard_map/all_to_all | solution.py:21
  110.7 19.6 %all-to-all-done = bf16[8,256,384]{2,1,0:T(8,128)(2,1)S(1)} async-done(((bf16[8,256,384]{2,1,0:T(8,128)(2,1)}), bf16[8,256,384]{2,1,0:T(8,128)(2,1)S(1)}, u32[]{:S(2)}, u32[]{:S(2)}) %all-to-all-start) | async-done | bytes 1572896 | tf_op jit(solution)/shard_map/all_to_all | solution.py:21
  131.4 4.3 all-to-all-start.1
  135.7 5.9 %all-to-all-done.1 = f32[16,256,1]{1,2,0:T(1,128)S(1)} async-done(((f32[16,256,1]{1,2,0:T(1,128)}), f32[16,256,1]{1,2,0:T(1,128)S(1)}, u32[]{:S(2)}, u32[]{:S(2)}) %all-to-all-start.1) | async-done | bytes 16416 | tf_op jit(solution)/shard_map/all_to_all | solution.py:27
  142.1 4.2 all_to_all.40
  146.4 12.0 %all_to_all.41 = bf16[4,2,1,1,96,384]{5,4,1,3,2,0:T(8,128)(2,1)S(1)} all-to-all(bf16[4,2,1,1,96,384]{5,4,1,3,2,0:T(8,128)(2,1)S(1)} %copy.51), channel_id=1, replica_groups=mesh['ctx'=8,'tp_0'=4,'tp_1'=2,'ep'=2] {'tp_0'}, dimensions={0} | all-to-all | bytes 1179648 | tf_op jit(solution)/shard_map/all_to_all | solution.py:45
  158.4 4.9 stack.3
  163.3 5.3 all-to-all-start.4
  168.8 14.5 %reshape_squeeze.11 = bf16[512,8,2,384]{3,2,1,0:T(2,128)(2,1)} reshape(bf16[1,512,6144]{2,1,0:T(8,128)(2,1)} %param.21) | data formatting | bytes 12582912 | tf_op jit(solution)/shard_map/reshape;squeeze | solution.py:145
  183.4 15.4 %constant_dynamic-slice_fusion.3 = (bf16[512,8,1,384]{3,2,1,0:T(2,128)(2,1)}, bf16[512,8,1,384]{3,2,1,0:T(2,128)(2,1)S(1)}) fusion(bf16[512,8,2,384]{3,2,1,0:T(2,128)(2,1)} %reshape_squeeze.11, s32[]{:T(128)S(6)} %select_n.93, s32[]{:T(128)S(6)} %select_n.94), kind=kLoop, calls=%fused_computation.93 | loop fusion | bytes 12582920 | tf_op jit(solution)/shard_map/jit(dynamic_index_in_dim)/dynamic_slice | solution.py:147
  198.8 2.9 copy.71
  201.6 1.3 collective-permute-start.1
  202.9 101.6 %all-to-all-done.4 = bf16[16,1,8,96,384]{4,3,2,1,0:T(8,128)(2,1)} async-done(((bf16[16,1,8,96,384]{4,3,2,1,0:T(8,128)(2,1)}), bf16[16,1,8,96,384]{4,3,2,1,0:T(8,128)(2,1)}, u32[]{:S(2)}, u32[]{:S(2)}) %all-to-all-start.4) | async-done | bytes 9437216 | tf_op jit(solution)/shard_map/all_to_all | solution.py:123
  305.0 88.4 %while.17 = (s32[]{:T(128)}, f32[8,96,512]{2,1,0:T(8,128)S(1)}, f32[8,96,512]{2,1,0:T(8,128)S(1)}, bf16[16,8,96,384]{3,2,1,0:T(8,128)(2,1)}, bf16[8,2,384,512]{3...) while((s32[]{:T(128)}, f32[8,96,512]{2,1,0:T(8,128)S(1)}, ...), condition=%wide.region_11.12_spmd, body=%wide.region_10.11_spmd.sunk | while | flops 604078080 | bytes 9045304 | solution.py:143
  305.0 2.7 fusion.102
  307.8 2.7 fusion.101
  310.5 2.7 fusion.102
  313.3 2.7 fusion.101
  316.1 2.7 fusion.102
  318.8 2.7 fusion.101
  321.6 2.7 fusion.102
  324.3 2.7 fusion.101
  327.1 2.7 fusion.102
  329.8 2.7 fusion.101
  332.6 2.7 fusion.102
  335.4 2.7 fusion.101
  338.2 2.7 fusion.102
  340.9 2.7 fusion.101
  343.7 2.7 fusion.102
  346.4 2.7 fusion.101
  349.2 2.7 fusion.102
  351.9 2.7 fusion.101
  354.7 2.7 fusion.102
  357.5 2.7 fusion.101
  360.3 2.7 fusion.102
  363.0 2.7 fusion.101
  365.8 2.7 fusion.102
  368.5 2.7 fusion.101
  371.3 2.7 fusion.102
  374.0 2.7 fusion.101
  376.8 2.7 fusion.102
  379.6 2.7 fusion.101
  382.4 2.7 fusion.102
  385.1 2.7 fusion.101
  387.9 2.7 fusion.102
  390.6 2.7 fusion.101
  394.6 3.9 copy.72
  398.5 11.8 %collective-permute-done = bf16[8,96,512]{2,1,0:T(8,128)(2,1)S(1)} collective-permute-done((bf16[8,96,512]{2,1,0:T(8,128)(2,1)S(1)}, bf16[8,96,512]{2,1,0:T(8,128)(2,1)S(1)}, u32[]{:S(2)}, u32[]{:S(2)}) %collective-permute-start) | collective-permute-done | bytes 786464 | tf_op jit(solution)/shard_map/ppermute | solution.py:55
  410.3 6.7 %fusion.48 = bf16[8,96,8,384]{3,1,2,0:T(8,128)(2,1)S(1)} fusion(bf16[512,8,384]{2,0,1:T(8,128)(2,1)} %collective-permute-done.1, bf16[512,8,384]{2,0,1:T(8,128)(2,1)S(1)} %bitcast.179, bf16[8,96,512]{2,1,0:T(8,128)(2,1)S(1)} %collective-permute-done, bf16[8,96,512]{2,1,0:T(8,128)(2,1)S(1)} %multiply_convert_fusion), kind=kOutput, calls=%fused_computation.40 | convolution fusion | flops 4849926144 | bytes 12582912 | tf_op jit(solution)/shard_map/csf,ftj->cstj/dot_general | solution.py:153
  417.0 1.9 copy.56
  418.9 3.3 copy.66
  422.2 88.1 %reduce-scatter.2.cloned.1.call-done = bf16[96,3072]{1,0:T(8,128)(2,1)} async-done(((bf16[768,3072]{1,0:T(8,128)(2,1)}), bf16[96,3072]{1,0:T(8,128)(2,1)}) %reduce-scatter.2.cloned.1.call-update) | async-done | bytes 589840 | tf_op jit(solution)/shard_map/reduce_scatter | solution.py:156
  512.3 6.1 %all-to-all-start.5 = ((bf16[1,96,8,384]{3,1,0,2:T(8,128)(2,1)}), bf16[1,96,8,384]{3,1,0,2:T(8,128)(2,1)S(1)}, u32[]{:S(2)}, u32[]{:S(2)}) async-start(bf16[1,96,8,384]{3,1,0,2:T(8,128)(2,1)} %copy.57), calls=%async_computation.6 | async-start | bytes 1179648 | tf_op jit(solution)/shard_map/all_to_all | solution.py:163
  518.5 10.0 %all-to-all-done.5 = bf16[1,96,8,384]{3,1,0,2:T(8,128)(2,1)S(1)} async-done(((bf16[1,96,8,384]{3,1,0,2:T(8,128)(2,1)}), bf16[1,96,8,384]{3,1,0,2:T(8,128)(2,1)S(1)}, u32[]{:S(2)}, u32[]{:S(2)}) %all-to-all-start.5) | async-done | bytes 589856 | tf_op jit(solution)/shard_map/all_to_all | solution.py:163
  528.5 1.2 fusion.51
  (64 shorter events, 9.1 us)
Async XLA Ops:
  6.5 92.4 %all-gather.2.cloned.1.call-start = ((), (), s32[]{:S(2)}) async-start(), calls=%async_computation.7 | async-start | bytes 5308416 | tf_op jit(solution)/shard_map/all_gather | solution.py:98
  102.7 7.1 %copy-start.3 = (s32[256,2]{0,1:T(2,128)S(1)}, s32[256,2]{0,1:T(2,128)}, u32[]{:S(2)}) copy-start(s32[256,2]{0,1:T(2,128)} %param.22) | copy-start | bytes 6148
  102.7 27.8 %copy-start = (bf16[256,384]{1,0:T(8,128)(2,1)S(1)}, bf16[256,384]{1,0:T(8,128)(2,1)}, u32[]{:S(2)}) copy-start(bf16[256,384]{1,0:T(8,128)(2,1)} %param.13) | copy-start | bytes 589828
  102.7 32.9 %copy-start.5 = (bf16[384]{0:T(512)(128)(2,1)S(1)}, bf16[384]{0:T(512)(128)(2,1)}, u32[]{:S(2)}) copy-start(bf16[384]{0:T(512)(128)(2,1)} %param.18) | copy-start | bytes 2308
  104.1 26.3 %all-to-all-start = ((bf16[8,256,384]{2,1,0:T(8,128)(2,1)}), bf16[8,256,384]{2,1,0:T(8,128)(2,1)S(1)}, u32[]{:S(2)}, u32[]{:S(2)}) async-start(bf16[8,256,384]{2,1,0:T(8,128)(2,1)} %bitcast.153), calls=%async_computation | async-start | bytes 3145728 | tf_op jit(solution)/shard_map/all_to_all | solution.py:21
  130.7 32.6 %copy-start.1 = (bf16[256,384]{1,0:T(8,128)(2,1)}, bf16[256,384]{1,0:T(8,128)(2,1)S(1)}, u32[]{:S(2)}) copy-start(bf16[256,384]{1,0:T(8,128)(2,1)S(1)} %get-tuple-element.198) | copy-start | bytes 589828
  131.4 10.2 %all-to-all-start.1 = ((f32[16,256,1]{1,2,0:T(1,128)}), f32[16,256,1]{1,2,0:T(1,128)S(1)}, u32[]{:S(2)}, u32[]{:S(2)}) async-start(f32[16,256,1]{1,2,0:T(1,128)} %broadcast_in_dim.96), calls=%async_computation.1 | async-start | bytes 32768 | tf_op jit(solution)/shard_map/all_to_all | solution.py:27
  163.3 141.2 %all-to-all-start.4 = ((bf16[16,1,8,96,384]{4,3,2,1,0:T(8,128)(2,1)}), bf16[16,1,8,96,384]{4,3,2,1,0:T(8,128)(2,1)}, u32[]{:S(2)}, u32[]{:S(2)}) async-start(bf16[16,1,8,96,384]{4,3,2,1,0:T(8,128)(2,1)} %stack.3), calls=%async_computation.4 | async-start | bytes 18874368 | tf_op jit(solution)/shard_map/all_to_all | solution.py:123
  168.6 341.7 %reduce-scatter.2.cloned.1.call-start = ((), (), s32[]{:S(2)}) async-start(), calls=%async_computation.8 | async-start | bytes 5308416 | tf_op jit(solution)/shard_map/reduce_scatter | solution.py:156
  201.6 196.9 %collective-permute-start.1 = (bf16[512,8,384]{2,0,1:T(8,128)(2,1)}, bf16[512,8,384]{2,0,1:T(8,128)(2,1)}, u32[]{:S(2)}, u32[]{:S(2)}) collective-permute-start(bf16[512,8,384]{2,0,1:T(8,128)(2,1)} %bitcast.150), channel_id=1, source_target_pairs={{0,1},{1,0},{2,3},{3,2},{4,5},{5,4},{6,7},{7,6},{8,9},{9,8},{10,11... | collective-permute-start | bytes 9437192 | tf_op jit(solution)/shard_map/ppermute | solution.py:55
  393.8 16.5 %collective-permute-start = (bf16[8,96,512]{2,1,0:T(8,128)(2,1)S(1)}, bf16[8,96,512]{2,1,0:T(8,128)(2,1)S(1)}, u32[]{:S(2)}, u32[]{:S(2)}) collective-permute-start(bf16[8,96,512]{2,1,0:T(8,128)(2,1)S(1)} %multiply_convert_fusion), channel_id=1, source_target_pairs={{0,1},{1,0},{2,3},{3,2},{4,5},{5,4},{6,7},{7,6},{8,9},{9,8},{10,11... | collective-permute-start | bytes 2359304 | tf_op jit(solution)/shard_map/ppermute | solution.py:55
  422.2 96.2 %copy-start.4 = (s32[256,2]{0,1:T(2,128)S(1)}, s32[256,2]{0,1:T(2,128)}, u32[]{:S(2)}) copy-start(s32[256,2]{0,1:T(2,128)} %param.23) | copy-start | bytes 6148
  422.2 106.3 %copy-start.2 = (bf16[256,384]{1,0:T(8,128)(2,1)S(1)}, bf16[256,384]{1,0:T(8,128)(2,1)}, u32[]{:S(2)}) copy-start(bf16[256,384]{1,0:T(8,128)(2,1)} %copy-done.1) | copy-start | bytes 589828
  512.3 16.2 %all-to-all-start.5 = ((bf16[1,96,8,384]{3,1,0,2:T(8,128)(2,1)}), bf16[1,96,8,384]{3,1,0,2:T(8,128)(2,1)S(1)}, u32[]{:S(2)}, u32[]{:S(2)}) async-start(bf16[1,96,8,384]{3,1,0,2:T(8,128)(2,1)} %copy.57), calls=%async_computation.6 | async-start | bytes 1179648 | tf_op jit(solution)/shard_map/all_to_all | solution.py:163
Sparse Core Ops, SparseCore 0:
  9.5 89.3 all-gather.1
  422.3 87.8 reduce-scatter.1
